TPU v7x, 16 devices: a whole 2x2x2 slice. The times are simulated.
16 devices in a mesh: req: 2 (over z), cp: 8 (over y, x, core).
Axes of the slice: x: 2, y: 2, z: 2, core: 2. Of those that a mesh axis runs over, the one named last changes fastest.
Arguments:
- x: bfloat16 [4096, 5120], P(('req', 'cp')), parts along dimension 0
- pos: int32 [4096], P(('req', 'cp')), parts along dimension 0
- g1: bfloat16 [2, 5120], replicated
- g2: bfloat16 [2, 5120], replicated
- wq: bfloat16 [2, 5120, 5120], replicated
- wk: bfloat16 [2, 5120, 5120], replicated
- wv: bfloat16 [2, 5120, 5120], replicated
- wo: bfloat16 [2, 5120, 5120], replicated
- w1: bfloat16 [2, 5120, 13696], replicated
- w3: bfloat16 [2, 5120, 13696], replicated
- w2: bfloat16 [2, 13696, 5120], replicated
Outputs:
- output 1: bfloat16 [4096, 5120], P(('req', 'cp')), parts along dimension 0
- output 2: bfloat16 [2, 4096, 40, 128], P(None, 'req', 'cp'), parts along dimension 1
- output 3: bfloat16 [2, 4096, 40, 128], P(None, 'req', 'cp'), parts along dimension 1
There are 2 independent parts. A program takes and returns all parts, laid end to end along the dimension named above; an argument that names none is the same for every part.
All inputs are finite; a program needn't handle non-finite values.
Results may differ from a plain program's by a relative error of at most 0.0183331.
Values are sent between devices in bfloat16 or wider.
A program may use at most 5 GiB of HBM per device.

v0:
```python
import jax
import jax.numpy as jnp
from jax import lax
from jax.sharding import PartitionSpec as P

HEAD = 128
F32 = jnp.float32
BF16 = jnp.bfloat16


def _norm(x, g):
    x32 = x.astype(F32)
    r = lax.rsqrt(jnp.mean(x32 * x32, axis=-1, keepdims=True) + 1e-5)
    return (x32 * r * g.astype(F32)).astype(BF16)


def _angles(pos):
    half = HEAD // 2
    inv = 1.0 / (10000.0 ** (jnp.arange(half, dtype=F32) * (2.0 / HEAD)))
    ang = pos.astype(F32)[..., None] * inv
    return jnp.cos(ang)[..., None, :], jnp.sin(ang)[..., None, :]


def _rope(t, c, sn):
    half = HEAD // 2
    t1, t2 = t[..., :half], t[..., half:]
    return jnp.concatenate([t1 * c - t2 * sn, t2 * c + t1 * sn], axis=-1)


def _attention(q, kg, vg, mask):
    def one(a):
        qh, kh, vh = a
        sc = jnp.einsum('qd,kd->qk', qh, kh, preferred_element_type=F32) * HEAD ** -0.5
        p = jax.nn.softmax(jnp.where(mask, sc, -jnp.inf), axis=-1).astype(BF16)
        return jnp.dot(p, vh, preferred_element_type=F32).astype(BF16)

    o = lax.map(one, (q.transpose(1, 0, 2), kg.transpose(1, 0, 2), vg.transpose(1, 0, 2)))
    return o.transpose(1, 0, 2).reshape(q.shape[0], -1)


def _natural(a, ncp):
    n, seq = a.shape[0], a.shape[1]
    a = a.reshape((n, ncp, 2, seq // (2 * ncp)) + a.shape[2:])
    a = jnp.concatenate([a[:, :, 0], a[:, ::-1, 1]], axis=1)
    return a.reshape((n, seq) + a.shape[3:])


def solution(mesh):
    ncp = mesh.shape['cp']
    act = P(('req', 'cp'), None)
    cache = P(None, 'req', 'cp', None)

    def body(x, pos, g1, g2, wq, wk, wv, wo, w1, w3, w2):
        s_dev = x.shape[0]
        nh = wq.shape[2] // HEAD
        pos_all = lax.all_gather(pos, 'cp', tiled=True)
        mask = pos_all[None, :] <= pos[:, None]
        c, sn = _angles(pos)
        kl, vl = [], []
        for l in range(wq.shape[0]):
            h = _norm(x, g1[l])
            q = _rope(jnp.dot(h, wq[l], preferred_element_type=F32).reshape(s_dev, nh, HEAD), c, sn).astype(BF16)
            k = _rope(jnp.dot(h, wk[l], preferred_element_type=F32).reshape(s_dev, nh, HEAD), c, sn).astype(BF16)
            v = jnp.dot(h, wv[l], preferred_element_type=F32).astype(BF16).reshape(s_dev, nh, HEAD)
            kg = lax.all_gather(k, 'cp', tiled=True)
            vg = lax.all_gather(v, 'cp', tiled=True)
            o = _attention(q, kg, vg, mask)
            x = (x.astype(F32) + jnp.dot(o, wo[l], preferred_element_type=F32)).astype(BF16)
            h2 = _norm(x, g2[l])
            u = (jax.nn.silu(jnp.dot(h2, w1[l], preferred_element_type=F32))
                 * jnp.dot(h2, w3[l], preferred_element_type=F32)).astype(BF16)
            x = (x.astype(F32) + jnp.dot(u, w2[l], preferred_element_type=F32)).astype(BF16)
            kl.append(k)
            vl.append(v)
        kc = _natural(lax.all_to_all(jnp.stack(kl), 'cp', 2, 1, tiled=True), ncp)
        vc = _natural(lax.all_to_all(jnp.stack(vl), 'cp', 2, 1, tiled=True), ncp)
        return x, kc, vc

    return jax.shard_map(body, mesh=mesh, in_specs=(act, P(('req', 'cp'))) + (P(),) * 9,
                         out_specs=(act, cache, cache), check_vma=False)
```

profile of v0, /device:TPU:0, one launch (start us, length us, event | category | flops | bytes accessed | tf_op | source)
XLA Modules:
  0.0 1739.0 jit_solution(1924292048470985282)
XLA Ops:
  12.1 68.2 %slice_bitcast_fusion = (bf16[5120,5120]{0,1:T(8,128)(2,1)}, bf16[5120,5120]{0,1:T(8,128)(2,1)}) fusion(bf16[2,5120,5120]{2,1,0:T(8,128)(2,1)} %param.20), kind=kLoop, calls=%fused_computation.62 | loop fusion | bytes 209715200 | tf_op jit(solution)/shard_map/dot_general | solution.py:63
  80.3 65.1 %copy.62 = bf16[5120,5120]{1,0:T(8,128)(2,1)} copy(bf16[5120,5120]{0,1:T(8,128)(2,1)} %get-tuple-element.194) | data formatting | bytes 104857600 | tf_op jit(solution)/shard_map/dot_general | solution.py:63
  145.4 68.2 %slice_bitcast_fusion.3 = (bf16[5120,5120]{0,1:T(8,128)(2,1)}, bf16[5120,5120]{0,1:T(8,128)(2,1)}) fusion(bf16[2,5120,5120]{2,1,0:T(8,128)(2,1)} %param.19), kind=kLoop, calls=%fused_computation.67 | loop fusion | bytes 209715200 | tf_op jit(solution)/shard_map/dot_general | solution.py:62
  213.7 70.0 %copy.61 = bf16[5120,5120]{1,0:T(8,128)(2,1)} copy(bf16[5120,5120]{0,1:T(8,128)(2,1)} %get-tuple-element.195) | data formatting | bytes 104857600 | tf_op jit(solution)/shard_map/dot_general | solution.py:62
  283.7 21.4 %fusion.140 = f32[256,40,128]{0,2,1:T(8,128)S(1)} fusion(bf16[40,128,5120]{2,1,0:T(8,128)(2,1)} %bitcast.244, bf16[256,5120]{1,0:T(8,128)(2,1)S(1)} %copy-done.12, f32[5120]{0:T(1024)S(1)} %bitcast.269, f32[256]{0:T(256)S(1)} %copy-done.26), kind=kOutput, calls=%fused_computation.129 | convolution fusion | flops 13427015680 | bytes 60314624 | tf_op jit(solution)/shard_map/dot_general | solution.py:63
  305.1 21.5 %fusion.142 = f32[256,40,128]{0,2,1:T(8,128)S(1)} fusion(bf16[40,128,5120]{2,1,0:T(8,128)(2,1)} %bitcast.247, bf16[256,5120]{1,0:T(8,128)(2,1)S(1)} %copy-done.12, f32[5120]{0:T(1024)S(1)} %bitcast.270, f32[256]{0:T(256)S(1)} %copy-done.26), kind=kOutput, calls=%fused_computation.131 | convolution fusion | flops 13427015680 | bytes 60314624 | tf_op jit(solution)/shard_map/dot_general | solution.py:62
  332.7 21.6 %fusion.102 = bf16[256,5120]{1,0:T(8,128)(2,1)S(1)} fusion(bf16[2,5120,5120]{2,1,0:T(8,128)(2,1)} %param.21, bf16[256,5120]{1,0:T(8,128)(2,1)} %param.15, f32[5120]{0:T(1024)S(1)} %bitcast.271, f32[256]{0:T(256)S(1)} %copy-done.26), kind=kOutput, calls=%fused_computation.98 | convolution fusion | flops 13428326400 | bytes 57693184 | tf_op jit(solution)/shard_map/dot_general | solution.py:64
  358.1 10.7 all-gather
  371.0 72.1 %all-gather.6.cloned.1.call-done = bf16[2048,40,128]{0,2,1:T(8,128)(2,1)} async-done(((bf16[256,40,128]{0,2,1:T(8,128)(2,1)}), bf16[2048,40,128]{0,2,1:T(8,128)(2,1)}) %all-gather.6.cloned.1.call-update) | async-done | bytes 20971536 | tf_op jit(solution)/shard_map/all_gather | solution.py:65
  443.1 106.1 %all-gather.8.cloned.1.call-done = bf16[2048,40,128]{2,0,1:T(8,128)(2,1)} async-done(((bf16[256,40,128]{2,0,1:T(8,128)(2,1)}), bf16[2048,40,128]{2,0,1:T(8,128)(2,1)}) %all-gather.8.cloned.1.call-update) | async-done | bytes 20971536 | tf_op jit(solution)/shard_map/all_gather | solution.py:66
  551.0 179.3 %while.22 = (s32[]{:T(128)}, bf16[40,256,128]{1,2,0:T(8,128)(2,1)}, bf16[40,256,128]{1,2,0:T(8,128)(2,1)}, bf16[40,2048,128]{1,2,0:T(8,128)(2,1)}, bf16[40,2048,...) while((s32[]{:T(128)}, bf16[40,256,128]{1,2,0:T(8,128)(2,1)}, ...), condition=%wide.region_4.5_spmd.clone, body=%wide.region_1.4_spmd.clone.sunk | while | flops 273186304 | bytes 7749717 | solution.py:37
  730.4 22.8 %fusion.121 = (f32[256]{0:T(256)S(1)}, bf16[256,5120]{1,0:T(8,128)(2,1)}) fusion(bf16[256,5120]{0,1:T(8,128)(2,1)} %bitcast.261, bf16[2,5120,5120]{2,1,0:T(8,128)(2,1)} %param.22, bf16[256,5120]{1,0:T(8,128)(2,1)S(1)} %copy-done.13), kind=kOutput, calls=%fused_computation.105 | convolution fusion | flops 13429637120 | bytes 60294144 | tf_op jit(solution)/shard_map/dot_general | solution.py:68
  753.3 55.0 %fusion.36 = f32[256,13696]{1,0:T(8,128)} fusion(bf16[2,5120,13696]{2,1,0:T(8,128)(2,1)} %param.23, bf16[256,5120]{1,0:T(8,128)(2,1)} %get-tuple-element.218, f32[5120]{0:T(1024)S(1)} %bitcast.267, f32[256]{0:T(256)S(1)} %add_rsqrt_fusion.2), kind=kOutput, calls=%fused_computation.44 | convolution fusion | flops 35908485120 | bytes 156914688 | tf_op jit(solution)/shard_map/dot_general | solution.py:70
  808.2 55.1 %fusion.67.clone.5.clone.5 = bf16[256,13696]{1,0:T(8,128)(2,1)} fusion(bf16[2,5120,13696]{2,1,0:T(8,128)(2,1)} %param.24, f32[256,13696]{1,0:T(8,128)} %fusion.36, bf16[256,5120]{1,0:T(8,128)(2,1)S(1)} %copy-done.29, f32[5120]{0:T(1024)S(1)} %bitcast.268, f32[256]{0:T(256)S(1)} %add_rsqrt_fusion.2), kind=kOutput, calls=%fused_computation.71.clone.clone.clone.clone.clone.clone.clone.clone.clone.2 | convolution fusion | flops 35929522176 | bytes 163927040 | tf_op jit(solution)/shard_map/dot_general | solution.py:71
  863.3 52.8 %fusion.124 = (f32[256]{0:T(256)S(1)}, bf16[256,5120]{1,0:T(8,128)(2,1)S(1)}) fusion(bf16[2,13696,5120]{2,1,0:T(8,128)(2,1)} %param.25, bf16[256,5120]{1,0:T(8,128)(2,1)} %get-tuple-element.218, bf16[256,13696]{1,0:T(8,128)(2,1)} %fusion.67.clone.5.clone.5), kind=kOutput, calls=%fused_computation.108 | convolution fusion | flops 35911106560 | bytes 152503296 | tf_op jit(solution)/shard_map/dot_general | solution.py:72
  916.1 21.7 %fusion.105 = bf16[256,5120]{1,0:T(8,128)(2,1)S(1)} fusion(bf16[2,5120,5120]{2,1,0:T(8,128)(2,1)} %param.21, bf16[256,5120]{1,0:T(8,128)(2,1)S(1)} %get-tuple-element.220, f32[5120]{0:T(1024)S(1)} %bitcast.264, f32[256]{0:T(256)S(1)} %add_rsqrt_fusion.1), kind=kOutput, calls=%fused_computation.99 | convolution fusion | flops 13428326400 | bytes 57693184 | tf_op jit(solution)/shard_map/dot_general | solution.py:64
  941.6 65.1 %copy.67 = bf16[5120,5120]{1,0:T(8,128)(2,1)} copy(bf16[5120,5120]{0,1:T(8,128)(2,1)} %get-tuple-element.196) | data formatting | bytes 104857600 | tf_op jit(solution)/shard_map/dot_general | solution.py:62
  1006.7 65.8 %copy.68 = bf16[5120,5120]{1,0:T(8,128)(2,1)} copy(bf16[5120,5120]{0,1:T(8,128)(2,1)} %get-tuple-element.193) | data formatting | bytes 104857600 | tf_op jit(solution)/shard_map/dot_general | solution.py:63
  1072.5 21.5 %fusion.138 = f32[256,40,128]{0,2,1:T(8,128)S(1)} fusion(bf16[40,128,5120]{2,1,0:T(8,128)(2,1)} %bitcast.246, bf16[256,5120]{1,0:T(8,128)(2,1)S(1)} %get-tuple-element.220, f32[5120]{0:T(1024)S(1)} %bitcast.265, f32[256]{0:T(256)S(1)} %add_rsqrt_fusion.1), kind=kOutput, calls=%fused_computation.127 | convolution fusion | flops 13427015680 | bytes 60314624 | tf_op jit(solution)/shard_map/dot_general | solution.py:62
  1094.1 21.7 %fusion.136 = f32[256,40,128]{0,2,1:T(8,128)S(1)} fusion(bf16[40,128,5120]{2,1,0:T(8,128)(2,1)} %bitcast.245, bf16[256,5120]{1,0:T(8,128)(2,1)S(1)} %get-tuple-element.220, f32[5120]{0:T(1024)S(1)} %bitcast.266, f32[256]{0:T(256)S(1)} %add_rsqrt_fusion.1), kind=kOutput, calls=%fused_computation.125 | convolution fusion | flops 13427015680 | bytes 60314624 | tf_op jit(solution)/shard_map/dot_general | solution.py:63
  1138.3 80.0 %all-to-all-done.1 = bf16[2,256,40,128]{3,1,0,2:T(8,128)(2,1)} async-done(((bf16[2,256,40,128]{3,1,0,2:T(8,128)(2,1)}), bf16[2,256,40,128]{3,1,0,2:T(8,128)(2,1)}, u32[]{:S(2)}, u32[]{:S(2)}) %all-to-all-start.1) | async-done | bytes 5242912 | tf_op jit(solution)/shard_map/all_to_all | solution.py:76
  1218.3 5.0 all-to-all-start
  1234.3 100.4 %all-to-all-done = bf16[2,256,40,128]{1,3,0,2:T(8,128)(2,1)} async-done(((bf16[2,256,40,128]{1,3,0,2:T(8,128)(2,1)}), bf16[2,256,40,128]{1,3,0,2:T(8,128)(2,1)}, u32[]{:S(2)}, u32[]{:S(2)}) %all-to-all-start) | async-done | bytes 5242912 | tf_op jit(solution)/shard_map/all_to_all | solution.py:75
  1334.7 8.3 reshape.195
  1343.0 13.4 fusion.166
  1356.3 11.1 copy.91
  1367.4 9.7 copy.90
  1382.2 155.4 %while.23 = (s32[]{:T(128)}, bf16[40,256,128]{1,2,0:T(8,128)(2,1)S(1)}, bf16[40,256,128]{1,2,0:T(8,128)(2,1)}, bf16[40,2048,128]{1,2,0:T(8,128)(2,1)}, bf16[40,2...) while((s32[]{:T(128)}, bf16[40,256,128]{1,2,0:T(8,128)(2,1)S(1)}, ...), condition=%wide.region_10.11_spmd.clone, body=%wide.region_7.10_spmd.clone.sunk | while | flops 273186304 | bytes 7749209 | solution.py:37
  1537.7 24.2 %fusion.127 = (f32[256]{0:T(256)S(1)}, bf16[256,5120]{1,0:T(8,128)(2,1)}) fusion(bf16[256,5120]{0,1:T(8,128)(2,1)S(1)} %bitcast.260, bf16[2,5120,5120]{2,1,0:T(8,128)(2,1)} %param.22, bf16[256,5120]{1,0:T(8,128)(2,1)} %copy-done.28), kind=kOutput, calls=%fused_computation.111 | convolution fusion | flops 13429637120 | bytes 60294144 | tf_op jit(solution)/shard_map/dot_general | solution.py:68
  1561.9 59.2 %fusion.30 = f32[256,13696]{1,0:T(8,128)} fusion(bf16[2,5120,13696]{2,1,0:T(8,128)(2,1)} %param.23, bf16[256,5120]{1,0:T(8,128)(2,1)} %get-tuple-element.222, f32[5120]{0:T(1024)S(1)} %bitcast.262, f32[256]{0:T(256)S(1)} %add_rsqrt_fusion), kind=kOutput, calls=%fused_computation.38 | convolution fusion | flops 35908485120 | bytes 156914688 | tf_op jit(solution)/shard_map/dot_general | solution.py:70
  1621.1 54.5 %fusion.62.clone.9 = bf16[256,13696]{1,0:T(8,128)(2,1)} fusion(bf16[2,5120,13696]{2,1,0:T(8,128)(2,1)} %param.24, f32[256,13696]{1,0:T(8,128)} %fusion.30, bf16[256,5120]{1,0:T(8,128)(2,1)S(1)} %copy-done.30, f32[5120]{0:T(1024)S(1)} %bitcast.263, f32[256]{0:T(256)S(1)} %add_rsqrt_fusion), kind=kOutput, calls=%fused_computation.70.clone.clone.clone.clone.clone.clone.clone.2 | convolution fusion | flops 35929522176 | bytes 163927040 | tf_op jit(solution)/shard_map/dot_general | solution.py:71
  1675.7 56.6 %fusion.113 = bf16[256,5120]{1,0:T(8,128)(2,1)} fusion(bf16[2,13696,5120]{2,1,0:T(8,128)(2,1)} %param.25, bf16[256,5120]{1,0:T(8,128)(2,1)S(1)} %copy-done.30, bf16[256,13696]{1,0:T(8,128)(2,1)} %fusion.62.clone.9), kind=kOutput, calls=%fused_computation.101 | convolution fusion | flops 35907174400 | bytes 152502272 | tf_op jit(solution)/shard_map/dot_general | solution.py:72
  (508 shorter events, 393.6 us)
Async XLA Ops:
  7.2 435.9 %all-gather.6.cloned.1.call-start = ((), (), s32[]{:S(2)}) async-start(), calls=%async_computation.2 | async-start | bytes 23592960 | tf_op jit(solution)/shard_map/all_gather | solution.py:65
  213.6 70.0 %copy-start.12 = (bf16[256,5120]{1,0:T(8,128)(2,1)S(1)}, bf16[256,5120]{1,0:T(8,128)(2,1)}, u32[]{:S(2)}) copy-start(bf16[256,5120]{1,0:T(8,128)(2,1)} %param.15) | copy-start | bytes 7864324
  213.6 70.0 %copy-start.21 = (f32[1,5120]{1,0:T(1,128)S(1)}, f32[1,5120]{1,0:T(1,128)}, u32[]{:S(2)}) copy-start(f32[1,5120]{1,0:T(1,128)} %get-tuple-element.214) | copy-start | bytes 61444
  213.7 70.0 %copy-start.26 = (f32[256]{0:T(256)S(1)}, f32[256]{0:T(256)}, u32[]{:S(2)}) copy-start(f32[256]{0:T(256)} %add_rsqrt_fusion.3) | copy-start | bytes 3076
  305.0 21.5 %copy-start.24 = (s32[256]{0:T(256)S(1)}, s32[256]{0:T(256)}, u32[]{:S(2)}) copy-start(s32[256]{0:T(256)} %param.16) | copy-start | bytes 3076
  305.0 21.5 %copy-start.27 = (f32[64]{0:T(128)S(1)}, f32[64]{0:T(128)}, u32[]{:S(2)}) copy-start(f32[64]{0:T(128)} %negate_power_fusion) | copy-start | bytes 772
  326.9 2.0 copy-start.14
  326.9 2.0 copy-start.16
  328.9 1.5 copy-start.2
  332.2 217.1 %all-gather.8.cloned.1.call-start = ((), (), s32[]{:S(2)}) async-start(), calls=%async_computation.3 | async-start | bytes 23592960 | tf_op jit(solution)/shard_map/all_gather | solution.py:66
  358.0 12.4 copy-start.18
  358.0 1023.9 %all-gather.12.cloned.1.call-start = ((), (), s32[]{:S(2)}) async-start(), calls=%async_computation.5 | async-start | bytes 23592960 | tf_op jit(solution)/shard_map/all_gather | solution.py:66
  551.0 179.3 %copy-start.13 = (bf16[256,5120]{1,0:T(8,128)(2,1)S(1)}, bf16[256,5120]{1,0:T(8,128)(2,1)}, u32[]{:S(2)}) copy-start(bf16[256,5120]{1,0:T(8,128)(2,1)} %param.15) | copy-start | bytes 7864324
  730.4 22.9 %copy-start.22 = (s32[2048]{0:T(1024)}, s32[2048]{0:T(1024)S(1)}, u32[]{:S(2)}) copy-start(s32[2048]{0:T(1024)S(1)} %get-tuple-element.381) | copy-start | bytes 24580
  753.3 55.0 %copy-start.29 = (bf16[256,5120]{1,0:T(8,128)(2,1)S(1)}, bf16[256,5120]{1,0:T(8,128)(2,1)}, u32[]{:S(2)}) copy-start(bf16[256,5120]{1,0:T(8,128)(2,1)} %get-tuple-element.218) | copy-start | bytes 7864324
  863.3 52.8 %copy-start.20 = (f32[1,5120]{1,0:T(1,128)S(1)}, f32[1,5120]{1,0:T(1,128)}, u32[]{:S(2)}) copy-start(f32[1,5120]{1,0:T(1,128)} %get-tuple-element.213) | copy-start | bytes 61444
  916.1 178.0 %copy-start.28 = (bf16[256,5120]{1,0:T(8,128)(2,1)}, bf16[256,5120]{1,0:T(8,128)(2,1)S(1)}, u32[]{:S(2)}) copy-start(bf16[256,5120]{1,0:T(8,128)(2,1)S(1)} %get-tuple-element.220) | copy-start | bytes 7864324
  941.5 440.3 %all-gather.10.cloned.1.call-start = ((), (), s32[]{:S(2)}) async-start(), calls=%async_computation.4 | async-start | bytes 23592960 | tf_op jit(solution)/shard_map/all_gather | solution.py:65
  1094.1 21.7 %copy-start.15 = (f32[256,64]{0,1:T(8,128)S(1)}, f32[256,64]{0,1:T(8,128)}, u32[]{:S(2)}) copy-start(f32[256,64]{0,1:T(8,128)} %copy-done.14) | copy-start | bytes 196612
  1094.1 21.7 %copy-start.17 = (f32[256,64]{0,1:T(8,128)S(1)}, f32[256,64]{0,1:T(8,128)}, u32[]{:S(2)}) copy-start(f32[256,64]{0,1:T(8,128)} %copy-done.16) | copy-start | bytes 196612
  1118.9 3.3 copy-start.7
  1122.1 1.7 copy-start.9
  1127.9 4.9 copy-start.1
  1127.9 5.0 copy-start.3
  1127.9 90.5 %all-to-all-start.1 = ((bf16[2,256,40,128]{3,1,0,2:T(8,128)(2,1)}), bf16[2,256,40,128]{3,1,0,2:T(8,128)(2,1)}, u32[]{:S(2)}, u32[]{:S(2)}) async-start(bf16[2,256,40,128]{3,1,0,2:T(8,128)(2,1)} %pad_maximum_fusion.1), calls=%async_computation.1 | async-start | bytes 10485760 | tf_op jit(solution)/shard_map/all_to_all | solution.py:76
  1138.3 85.1 %copy-start.10 = (bf16[256,40,64]{0,2,1:T(8,128)(2,1)S(1)}, bf16[256,40,64]{0,2,1:T(8,128)(2,1)}, u32[]{:S(2)}) copy-start(bf16[256,40,64]{0,2,1:T(8,128)(2,1)} %get-tuple-element.207) | copy-start | bytes 3932164
  1138.3 85.1 %copy-start.11 = (bf16[256,40,64]{0,2,1:T(8,128)(2,1)S(1)}, bf16[256,40,64]{0,2,1:T(8,128)(2,1)}, u32[]{:S(2)}) copy-start(bf16[256,40,64]{0,2,1:T(8,128)(2,1)} %get-tuple-element.208) | copy-start | bytes 3932164
  1218.3 116.4 %all-to-all-start = ((bf16[2,256,40,128]{1,3,0,2:T(8,128)(2,1)}), bf16[2,256,40,128]{1,3,0,2:T(8,128)(2,1)}, u32[]{:S(2)}, u32[]{:S(2)}) async-start(bf16[2,256,40,128]{1,3,0,2:T(8,128)(2,1)} %copy.73), calls=%async_computation | async-start | bytes 10485760 | tf_op jit(solution)/shard_map/all_to_all | solution.py:75
  1379.0 3.1 copy-start.23
  1379.0 3.1 copy-start.25
  1537.7 24.3 %copy-start.19 = (f32[1,5120]{1,0:T(1,128)S(1)}, f32[1,5120]{1,0:T(1,128)}, u32[]{:S(2)}) copy-start(f32[1,5120]{1,0:T(1,128)} %get-tuple-element.211) | copy-start | bytes 61444
  1561.9 59.2 %copy-start.30 = (bf16[256,5120]{1,0:T(8,128)(2,1)S(1)}, bf16[256,5120]{1,0:T(8,128)(2,1)}, u32[]{:S(2)}) copy-start(bf16[256,5120]{1,0:T(8,128)(2,1)} %get-tuple-element.222) | copy-start | bytes 7864324
  (5 other events, 6.6 us)
Sparse Core Ops, SparseCore 0:
  332.3 110.7 all-gather.5
  445.5 103.6 all-gather.7
  941.7 103.6 all-gather.11
  1122.3 212.2 all-gather.9
where the time goes:
time: 1760 us; the launch traced here: 1740 us
  matrix products  773 us (44%)
  local copies, waits for them, and re-layouts  508 us (29%)
  waiting for transfers between devices  359 us (20%)
  other arithmetic  61.5 us (3%)
    dot_general x3, local copies, waits for them, and re-layouts, body(): jnp.dot(h, wq[l], preferred_element_type=F32).reshape(s_dev, nh, HEAD)  203 us
    dot_general x3, local copies, waits for them, and re-layouts, body(): jnp.dot(h, wk[l], preferred_element_type=F32).reshape(s_dev, nh, HEAD)  199 us
    dot_general x80, matrix products, one(): jnp.einsum('qd,kd->qk', qh, kh, preferred_element_type=F32) * HEAD ** (-0.5)  132 us
    dot_general x80, matrix products, one(): return jnp.dot(p, vh, preferred_element_type=F32).astype(BF16)  131 us
    dot_general x2, matrix products, body(): jnp.dot(h2, w1[l], preferred_element_type=F32)  114 us
    dot_general x2, matrix products, body(): jnp.dot(h2, w3[l], preferred_element_type=F32)  110 us
    dot_general x2, matrix products, body(): jnp.dot(u, w2[l], preferred_element_type=F32)  109 us
    all_gather x2, waiting for transfers between devices, body(): vg = lax.all_gather(v, 'cp', tiled=True)  106 us
  transfers between devices with their start and end apart: 6, of which 4 were waited for; matrix products, arithmetic and copies ran while one was open for 16% of the time, Pallas kernels for 0%

commit v1 on v0

v1 whole, which is shorter than its diff:
```python
import functools

import jax
import jax.numpy as jnp
from jax import lax
from jax.experimental import pallas as pl
from jax.experimental.pallas import tpu as pltpu
from jax.sharding import PartitionSpec as P

HEAD = 128
F32 = jnp.float32
BF16 = jnp.bfloat16
MESH = pl.DeviceIdType.MESH
ANY = pl.BlockSpec(memory_space=pl.ANY)
VM = pl.BlockSpec(memory_space=pltpu.VMEM)
NCP = 8
VLIM = 62 * 1024 * 1024


def _tables(pos):
    half = HEAD // 2
    inv = 1.0 / (10000.0 ** (jnp.arange(half, dtype=F32) * (2.0 / HEAD)))
    ang = pos.astype(F32)[:, None] * inv
    c, s = jnp.cos(ang), jnp.sin(ang)
    return jnp.concatenate([c, c], axis=-1), jnp.concatenate([-s, s], axis=-1)


def _norm(x, g):
    x32 = x.astype(F32)
    r = lax.rsqrt(jnp.mean(x32 * x32, axis=-1, keepdims=True) + 1e-5)
    return (x32 * r * g.astype(F32)).astype(BF16)


def _me():
    me = lax.axis_index('cp')
    return me, me // 4, (me // 2) % 2, me % 2


def _peer(p):
    _, y, x, c = _me()
    return ((y + p // 4) % 2) * 4 + ((x + (p // 2) % 2) % 2) * 2 + (c + p % 2) % 2


def _greet():
    barrier = pltpu.get_barrier_semaphore()
    for p in range(1, NCP):
        pl.semaphore_signal(barrier, inc=1, device_id={'cp': _peer(p)}, device_id_type=MESH)
    pl.semaphore_wait(barrier, NCP - 1)


def _rows(dev, half, seg):
    return pl.multiple_of((dev + half * (2 * NCP - 1 - 2 * dev)) * seg, seg)


def _qkv_kernel(l, x_hbm, g_ref, c_ref, s_ref, wk, wv, wq, k_out, v_out, q_out,
                x_ref, h_ref, wbuf, obuf, xsem, wsem, send, recv, own):
    me = _me()[0]
    wd = wbuf.shape[2]
    seg = x_ref.shape[0] // 2
    nh = wd // HEAD
    nb = wbuf.shape[0]
    ws, outs = (wk, wv, wq), (k_out, v_out, q_out)

    def wcopy(m, j):
        d = _peer(NCP - 1 - j)
        slot = (m * NCP + j) % nb
        return pltpu.make_async_copy(ws[m].at[l, :, pl.ds(pl.multiple_of(d * wd, wd), wd)],
                                     wbuf.at[slot], wsem.at[slot])

    def tile(m, p, half):
        return (obuf.at[m, p, :, pl.ds(half * seg, seg)],
                outs[m].at[:, pl.ds(_rows(me, half, seg), seg)])

    def remote(m, p, half):
        src, dst = tile(m, p, half)
        return pltpu.make_async_remote_copy(
            src_ref=src, dst_ref=dst, send_sem=send.at[m, p, half], recv_sem=recv.at[m, p, half],
            device_id={'cp': _peer(p)}, device_id_type=MESH)

    def local(m, half):
        src, dst = tile(m, 0, half)
        return pltpu.make_async_copy(src, dst, own.at[m, half])

    xcp = pltpu.make_async_copy(x_hbm, x_ref, xsem)
    xcp.start()
    for j in range(nb - 1):
        wcopy(0, j).start()
    _greet()
    xcp.wait()
    h_ref[...] = _norm(x_ref[...], g_ref[...])

    for m in range(3):
        def step(j, _):
            ahead = nb - 1

            @pl.when(j < NCP - ahead)
            def _():
                wcopy(m, j + ahead).start()
            if m < 2:
                @pl.when(j >= NCP - ahead)
                def _():
                    wcopy(m + 1, j + ahead - NCP).start()
            wcopy(m, j).wait()
            p = NCP - 1 - j
            acc = jnp.dot(h_ref[...], wbuf[(m * NCP + j) % nb], preferred_element_type=F32)
            for h in range(nh):
                t = acc[:, h * HEAD:(h + 1) * HEAD]
                if m != 1:
                    t = t * c_ref[...] + pltpu.roll(t, HEAD // 2, 1) * s_ref[...]
                obuf[m, p, h] = t.astype(BF16)

            @pl.when(p > 0)
            def _():
                for half in range(2):
                    remote(m, p, half).start()

            @pl.when(p == 0)
            def _():
                for half in range(2):
                    local(m, half).start()
            return 0

        lax.fori_loop(0, NCP, step, 0)

    for m in range(3):
        for half in range(2):
            local(m, half).wait()

        def fin(p, _):
            for half in range(2):
                remote(m, p, half).wait()
            return 0

        lax.fori_loop(1, NCP, fin, 0)


def _qkv(x, g, c, s, wk, wv, wq, l):
    rows, d = x.shape
    wd = wq.shape[2] // NCP
    nh, nb = wd // HEAD, 3
    out = jax.ShapeDtypeStruct((nh, rows * NCP, HEAD), BF16)
    return pl.pallas_call(
        functools.partial(_qkv_kernel, l),
        in_specs=[ANY, VM, VM, VM, ANY, ANY, ANY],
        out_specs=[ANY] * 3,
        out_shape=[out] * 3,
        scratch_shapes=[
            pltpu.VMEM((rows, d), BF16), pltpu.VMEM((rows, d), BF16),
            pltpu.VMEM((nb, d, wd), BF16), pltpu.VMEM((3, NCP, nh, rows, HEAD), BF16),
            pltpu.SemaphoreType.DMA, pltpu.SemaphoreType.DMA((nb,)),
            pltpu.SemaphoreType.DMA((3, NCP, 2)), pltpu.SemaphoreType.DMA((3, NCP, 2)),
            pltpu.SemaphoreType.DMA((3, 2)),
        ],
        compiler_params=pltpu.CompilerParams(
            vmem_limit_bytes=VLIM, collective_id=2 * l, has_side_effects=True),
        name=f'qkv{l}',
    )(x, g, c, s, wk, wv, wq)


def _attn_kernel(q_ref, k_ref, v_ref, o_out, obuf, acc_ref, send, recv, own):
    me = _me()[0]
    n, bq, wd = obuf.shape
    nh = wd // HEAD
    seg = o_out.shape[0] // 2
    per = bq // seg
    nseg = n * per
    cexp = HEAD ** -0.5 * 1.4426950408889634
    dmask = (lax.broadcasted_iota(jnp.int32, (bq, bq), 0)
             <= lax.broadcasted_iota(jnp.int32, (bq, bq), 1))

    def half_of(sg):
        return sg // NCP

    def owner(sg):
        return sg + half_of(sg) * (2 * NCP - 1 - 2 * sg)

    def place(dev, half):
        return o_out.at[pl.ds(pl.multiple_of(half * seg, seg), seg),
                        pl.ds(pl.multiple_of(dev * wd, wd), wd)]

    def remote(sg):
        return pltpu.make_async_remote_copy(
            src_ref=obuf.at[sg // per, pl.ds(pl.multiple_of((sg % per) * seg, seg), seg)],
            dst_ref=place(me, half_of(sg)),
            send_sem=send.at[sg], recv_sem=recv.at[me, half_of(sg)],
            device_id={'cp': owner(sg)}, device_id_type=MESH)

    def local(sg):
        return pltpu.make_async_copy(
            obuf.at[sg // per, pl.ds(pl.multiple_of((sg % per) * seg, seg), seg)],
            place(me, half_of(sg)), own.at[half_of(sg)])

    _greet()

    def qblock(qi, _):
        qrows = pl.ds(pl.multiple_of(qi * bq, bq), bq)
        acc_ref[...] = jnp.zeros_like(acc_ref)

        def block(kb, carry, diag):
            rows = pl.ds(pl.multiple_of(kb * bq, bq), bq)
            new = []
            for h in range(nh):
                m, den = carry[h]
                sc = lax.dot_general(k_ref[h, rows], q_ref[h, qrows], (((1,), (1,)), ((), ())),
                                     preferred_element_type=F32)
                if diag:
                    sc = jnp.where(dmask, sc, -jnp.inf)
                mn = jnp.maximum(m, jnp.max(sc, axis=0, keepdims=True))
                p = jnp.exp2((sc - mn) * cexp)
                al = jnp.exp2((m - mn) * cexp)
                den = den * al + jnp.sum(p, axis=0, keepdims=True)
                pv = lax.dot_general(v_ref[h, rows], p.astype(BF16), (((0,), (0,)), ((), ())),
                                     preferred_element_type=F32)
                acc_ref[h] = acc_ref[h] * al + pv
                new.append((mn, den))
            return tuple(new)

        init = tuple((jnp.full((1, bq), -jnp.inf, F32), jnp.zeros((1, bq), F32)) for _ in range(nh))
        carry = block(qi, init, True)
        carry = lax.fori_loop(0, qi, lambda kb, cr: block(kb, cr, False), carry)
        for h in range(nh):
            obuf[qi, :, h * HEAD:(h + 1) * HEAD] = (acc_ref[h] / carry[h][1]).T.astype(BF16)

        def push(i, _):
            sg = qi * per + i

            @pl.when(owner(sg) != me)
            def _():
                remote(sg).start()

            @pl.when(owner(sg) == me)
            def _():
                local(sg).start()
            return 0

        lax.fori_loop(0, per, push, 0)
        return 0

    lax.fori_loop(0, n, qblock, 0)

    def fin_send(sg, _):
        @pl.when(owner(sg) != me)
        def _():
            remote(sg).wait_send()

        @pl.when(owner(sg) == me)
        def _():
            local(sg).wait()
        return 0

    lax.fori_loop(0, nseg, fin_send, 0)

    def fin_recv(p, _):
        src = _peer(p)
        for half in range(2):
            pltpu.make_async_remote_copy(
                src_ref=obuf.at[0, pl.ds(0, seg)], dst_ref=place(src, half),
                send_sem=send.at[0], recv_sem=recv.at[src, half],
                device_id={'cp': src}, device_id_type=MESH).wait_recv()
        return 0

    lax.fori_loop(1, NCP, fin_recv, 0)


def _attn(q, k, v, l):
    nh, n, _ = q.shape
    wd, bq = nh * HEAD, 512
    return pl.pallas_call(
        _attn_kernel,
        in_specs=[VM] * 3,
        out_specs=ANY,
        out_shape=jax.ShapeDtypeStruct((n // NCP, wd * NCP), BF16),
        scratch_shapes=[
            pltpu.VMEM((n // bq, bq, wd), BF16), pltpu.VMEM((nh, HEAD, bq), F32),
            pltpu.SemaphoreType.DMA((2 * NCP,)), pltpu.SemaphoreType.DMA((NCP, 2)),
            pltpu.SemaphoreType.DMA((2,)),
        ],
        compiler_params=pltpu.CompilerParams(
            vmem_limit_bytes=VLIM, collective_id=2 * l + 1, has_side_effects=True),
        name=f'attn{l}',
    )(q, k, v)


def _mlp_kernel(l, o_hbm, x_hbm, g_ref, wo, w1, w3, w2, y_ref,
                o_ref, x_ref, h_ref, u_ref, wbuf, dbuf, asem, wsem, dsem):
    d = x_ref.shape[1]
    ff = u_ref.shape[1]
    tn = wbuf.shape[2] // 2
    nb, nd = wbuf.shape[0], dbuf.shape[0]
    n_o, n_up, n_dn = d // (2 * tn), pl.cdiv(ff, tn), d // tn

    def at(w, off):
        return w.at[l, :, pl.ds(pl.multiple_of(off, HEAD), tn)]

    def up_off(j):
        return jnp.minimum(j * tn, ff - tn)

    def pair(i, a, b):
        s = i % nb
        return (pltpu.make_async_copy(a, wbuf.at[s, :, pl.ds(0, tn)], wsem.at[s, 0]),
                pltpu.make_async_copy(b, wbuf.at[s, :, pl.ds(tn, tn)], wsem.at[s, 1]))

    def o_pair(j):
        return pair(j, at(wo, 2 * j * tn), at(wo, (2 * j + 1) * tn))

    def up_pair(j):
        return pair(n_o + j, at(w1, up_off(j)), at(w3, up_off(j)))

    def dn(j):
        s = j % nd
        return pltpu.make_async_copy(at(w2, j * tn), dbuf.at[s], dsem.at[s])

    def start(ps):
        for c in ps:
            c.start()

    def wait(ps):
        for c in ps:
            c.wait()

    acts = (pltpu.make_async_copy(o_hbm, o_ref, asem.at[0]),
            pltpu.make_async_copy(x_hbm, x_ref, asem.at[1]))
    start(acts)
    ahead = nb - 1
    for j in range(ahead):
        start(o_pair(j))
    wait(acts)

    def o_step(j, _):
        @pl.when(j + ahead < n_o)
        def _():
            start(o_pair(j + ahead))

        @pl.when(j + ahead >= n_o)
        def _():
            start(up_pair(j + ahead - n_o))
        wait(o_pair(j))
        cs = pl.ds(pl.multiple_of(2 * j * tn, tn), 2 * tn)
        x_ref[:, cs] = (x_ref[:, cs].astype(F32)
                        + jnp.dot(o_ref[...], wbuf[j % nb], preferred_element_type=F32)).astype(BF16)
        return 0

    lax.fori_loop(0, n_o, o_step, 0)
    h_ref[...] = _norm(x_ref[...], g_ref[...])

    def up_step(j, _):
        @pl.when(j + ahead < n_up)
        def _():
            start(up_pair(j + ahead))

        @pl.when(j == n_up - 4)
        def _():
            for i in range(nd - 1):
                dn(i).start()
        wait(up_pair(j))
        ab = jnp.dot(h_ref[...], wbuf[(n_o + j) % nb], preferred_element_type=F32)
        a, b = ab[:, :tn], ab[:, tn:]
        u_ref[:, pl.ds(pl.multiple_of(up_off(j), HEAD), tn)] = (jax.nn.silu(a) * b).astype(BF16)
        return 0

    lax.fori_loop(0, n_up, up_step, 0)

    def dn_step(j, _):
        @pl.when(j + nd - 1 < n_dn)
        def _():
            dn(j + nd - 1).start()
        dn(j).wait()
        cs = pl.ds(pl.multiple_of(j * tn, tn), tn)
        y_ref[:, cs] = (x_ref[:, cs].astype(F32)
                        + jnp.dot(u_ref[...], dbuf[j % nd], preferred_element_type=F32)).astype(BF16)
        return 0

    lax.fori_loop(0, n_dn, dn_step, 0)


def _mlp(o, x, g, wo, w1, w3, w2, l):
    rows, d = x.shape
    ff = w1.shape[2]
    tn, nb, nd = 256, 3, 3
    return pl.pallas_call(
        functools.partial(_mlp_kernel, l),
        in_specs=[ANY, ANY, VM, ANY, ANY, ANY, ANY],
        out_specs=VM,
        out_shape=jax.ShapeDtypeStruct((rows, d), BF16),
        scratch_shapes=[
            pltpu.VMEM((rows, d), BF16), pltpu.VMEM((rows, d), BF16), pltpu.VMEM((rows, d), BF16),
            pltpu.VMEM((rows, ff), BF16), pltpu.VMEM((nb, d, 2 * tn), BF16), pltpu.VMEM((nd, ff, tn), BF16),
            pltpu.SemaphoreType.DMA((2,)), pltpu.SemaphoreType.DMA((nb, 2)), pltpu.SemaphoreType.DMA((nd,)),
        ],
        compiler_params=pltpu.CompilerParams(vmem_limit_bytes=VLIM),
        name=f'mlp{l}',
    )(o, x, g, wo, w1, w3, w2)


def solution(mesh):
    act = P(('req', 'cp'), None)
    cache = P(None, 'req', 'cp', None)

    def body(x, pos, g1, g2, wq, wk, wv, wo, w1, w3, w2):
        c, s = _tables(pos)
        ks, vs = [], []
        for l in range(wq.shape[0]):
            k, v, q = _qkv(x, g1[l:l + 1], c, s, wk, wv, wq, l)
            o = _attn(q, k, v, l)
            x = _mlp(o, x, g2[l:l + 1], wo, w1, w3, w2, l)
            ks.append(k)
            vs.append(v)
        return x, jnp.stack(ks).transpose(0, 2, 1, 3), jnp.stack(vs).transpose(0, 2, 1, 3)

    return jax.shard_map(body, mesh=mesh, in_specs=(act, P(('req', 'cp'))) + (P(),) * 9,
                         out_specs=(act, cache, cache), check_vma=False)
```

time: 1760 us -> 608 us (0.35); the launches traced: 1740 us -> 608 us
  matrix products: 773 us -> 0 us
  Pallas kernels: 0 us -> 594 us
  local copies, waits for them, and re-layouts: 508 us -> 2.9 us
  waiting for transfers between devices: 359 us -> 0 us
  other arithmetic: 61.5 us -> 10.4 us
    dot_general x174 -> x0, matrix products: 773 us -> none  [the longest x80 132 us: one(): jnp.einsum('qd,kd->qk', qh, kh, preferred_element_type=F32) * HEAD ** (-0.5)]
    pallas_call x0 -> x6, Pallas kernels: none -> 594 us  [the longest x2 305 us: _mlp(): pl.pallas_call(functools.partial(_mlp_kernel, l), in_specs=[ANY, ANY, VM,...]
    dot_general x6 -> x0, local copies, waits for them, and re-layouts: 402 us -> none  [the longest x3 203 us: body(): jnp.dot(h, wq[l], preferred_element_type=F32).reshape(s_dev, nh, HEAD)]
    all_to_all x2 -> x0, waiting for transfers between devices: 180 us -> none  [the longest x1 100 us: body(): kc = _natural(lax.all_to_all(jnp.stack(kl), 'cp', 2, 1, tiled=True), ncp)]
    all_gather x4 -> x0, waiting for transfers between devices: 178 us -> none  [the longest x2 106 us: body(): vg = lax.all_gather(v, 'cp', tiled=True)]
    reduce_sum x81 -> x0, other arithmetic: 37.2 us -> none  [the longest x80 34.9 us: one(): p = jax.nn.softmax(jnp.where(mask, sc, -jnp.inf), axis=-1).astype(BF16)]
    dynamic_update_slice x160 -> x0, local copies, waits for them, and re-layouts: 34.6 us -> none  [_attention(): lax.map(one, (q.transpose(1, 0, 2), kg.transpose(1, 0, 2), vg.transpose(1...]
    unnamed x66 -> x4, local copies, waits for them, and re-layouts: 28.4 us -> 0.01 us
  transfers between devices with their start and end apart: 6 -> 0, of which waited for: 4 -> 0; matrix products, arithmetic and copies ran while one was open for 16% -> 0% of each run, Pallas kernels for 0% -> 0%
where the time goes in v1:
time: 608 us
  Pallas kernels  594 us (98%)
  other arithmetic  10.4 us (2%)
    pallas_call x2, Pallas kernels, _mlp(): pl.pallas_call(functools.partial(_mlp_kernel, l), in_specs=[ANY, ANY, VM,...  305 us
    pallas_call x2, Pallas kernels, _qkv(): pl.pallas_call(functools.partial(_qkv_kernel, l), in_specs=[ANY, VM, VM,...  193 us
    pallas_call x2, Pallas kernels, _attn(): pl.pallas_call(_attn_kernel, in_specs=[VM] * 3, out_specs=ANY, out_shape=...  95.9 us

profile of v1, /device:TPU:0, one launch (start us, length us, event | category | flops | bytes accessed | tf_op | source)
XLA Modules:
  0.0 608.0 jit_solution(13482400686220603738)
XLA Ops:
  0.6 0.7 convert_element_type.3
  1.3 1.4 fusion.2
  2.8 1.4 fusion.1
  4.2 0.5 fusion
  4.8 0.8 pad_maximum_fusion
  5.6 98.8 %qkv0.1 = (bf16[5,2048,128]{2,1,0:T(8,128)(2,1)}, bf16[5,2048,128]{2,1,0:T(8,128)(2,1)}, bf16[5,2048,128]{2,1,0:T(8,128)(2,1)}) custom-call(bf16[256,5120]{1,0:T(8,128)(2,1)} %x_hbm.3, bf16[1,5120]{1,0:T(2,128)(2,1)} %get-tuple-element.18.g_ref, f32[256,128]{1,0:T(8,128)} %get-tuple-element.22.c_ref, f32[256,128]{1,0:T(8,128)} %get-tuple-element.23.s_ref, ...), custom_call_target="tpu_custom_call" | custom-call | tf_op jit(solution)/shard_map/qkv0/pallas_call | solution.py:142
  104.4 47.5 %attn0.1.o_hbm = bf16[256,5120]{1,0:T(8,128)(2,1)} custom-call(bf16[5,2048,128]{2,1,0:T(8,128)(2,1)} %get-tuple-element.9.q_ref, bf16[5,2048,128]{2,1,0:T(8,128)(2,1)} %get-tuple-element.10.k_ref, bf16[5,2048,128]{2,1,0:T(8,128)(2,1)} %get-tuple-element.11.v_ref), custom_call_target="tpu_custom_call" | custom-call | tf_op jit(solution)/shard_map/attn0/pallas_call | solution.py:268
  152.0 153.4 %mlp0.1.x_hbm = bf16[256,5120]{1,0:T(8,128)(2,1)} custom-call(bf16[256,5120]{1,0:T(8,128)(2,1)} %attn0.1.o_hbm, bf16[256,5120]{1,0:T(8,128)(2,1)} %x_hbm.3, bf16[1,5120]{1,0:T(2,128)(2,1)} %get-tuple-element.16.g_ref, bf16[2,5120,5120]{2,1,0:T(8,128)(2,1)} %wo.3, bf16[2,5120,13696]{2,1,0:T(8,128)(2,1)} %w1.3, bf16[2,5120,13696]{2,1,0:T(8,128)(2,1)} %w3.3, ...), custom_call_target="tpu_custom_call" | custom-call | tf_op jit(solution)/shard_map/mlp0/pallas_call | solution.py:380
  305.4 93.9 %qkv1.1 = (bf16[5,2048,128]{2,1,0:T(8,128)(2,1)}, bf16[5,2048,128]{2,1,0:T(8,128)(2,1)}, bf16[5,2048,128]{2,1,0:T(8,128)(2,1)}) custom-call(bf16[256,5120]{1,0:T(8,128)(2,1)} %mlp0.1.x_hbm, bf16[1,5120]{1,0:T(2,128)(2,1)} %get-tuple-element.17.g_ref, f32[256,128]{1,0:T(8,128)} %get-tuple-element.22.c_ref, f32[256,128]{1,0:T(8,128)} %get-tuple-element.23.s_ref, ...), custom_call_target="tpu_custom_call" | custom-call | tf_op jit(solution)/shard_map/qkv1/pallas_call | solution.py:142
  399.3 48.4 %attn1.1.o_hbm = bf16[256,5120]{1,0:T(8,128)(2,1)} custom-call(bf16[5,2048,128]{2,1,0:T(8,128)(2,1)} %get-tuple-element.12.q_ref, bf16[5,2048,128]{2,1,0:T(8,128)(2,1)} %get-tuple-element.13.k_ref, bf16[5,2048,128]{2,1,0:T(8,128)(2,1)} %get-tuple-element.14.v_ref), custom_call_target="tpu_custom_call" | custom-call | tf_op jit(solution)/shard_map/attn1/pallas_call | solution.py:268
  447.7 152.0 %mlp1.1 = bf16[256,5120]{1,0:T(8,128)(2,1)} custom-call(bf16[256,5120]{1,0:T(8,128)(2,1)} %attn1.1.o_hbm, bf16[256,5120]{1,0:T(8,128)(2,1)} %mlp0.1.x_hbm, bf16[1,5120]{1,0:T(2,128)(2,1)} %get-tuple-element.15.g_ref, bf16[2,5120,5120]{2,1,0:T(8,128)(2,1)} %wo.3, bf16[2,5120,13696]{2,1,0:T(8,128)(2,1)} %w1.3, bf16[2,5120,13696]{2,1,0:T(8,128)(2,1)} %w3.3, ...), custom_call_target="tpu_custom_call" | custom-call | tf_op jit(solution)/shard_map/mlp1/pallas_call | solution.py:380
  599.7 0.0 copy-start
  599.7 0.0 copy-start.1
  599.7 5.5 maximum_bitcast_fusion
  605.2 0.0 copy-done
  605.2 0.0 copy-done.1
  605.2 2.8 maximum_bitcast_fusion.1
  (1 shorter events, 0.0 us)
Async XLA Ops:
  599.7 5.5 copy-start
  599.7 5.5 copy-start.1

commit v2 on v0

v2 whole, which is shorter than its diff:
```python
import functools

import jax
import jax.numpy as jnp
from jax import lax
from jax.experimental import pallas as pl
from jax.experimental.pallas import tpu as pltpu
from jax.sharding import PartitionSpec as P

HEAD = 128
F32 = jnp.float32
BF16 = jnp.bfloat16
MESH = pl.DeviceIdType.MESH
ANY = pl.BlockSpec(memory_space=pl.ANY)
VM = pl.BlockSpec(memory_space=pltpu.VMEM)
NCP = 8
BQ = 512
VLIM = 62 * 1024 * 1024


def _tables(pos):
    half = HEAD // 2
    inv = 1.0 / (10000.0 ** (jnp.arange(half, dtype=F32) * (2.0 / HEAD)))
    ang = pos.astype(F32)[:, None] * inv
    c, s = jnp.cos(ang), jnp.sin(ang)
    return jnp.concatenate([c, c], axis=-1), jnp.concatenate([-s, s], axis=-1)


def _norm(x, g):
    x32 = x.astype(F32)
    r = lax.rsqrt(jnp.mean(x32 * x32, axis=-1, keepdims=True) + 1e-5)
    return (x32 * r * g.astype(F32)).astype(BF16)


def _peer(p):
    me = lax.axis_index('cp')
    y, x, c = me // 4, (me // 2) % 2, me % 2
    return ((y + p // 4) % 2) * 4 + ((x + (p // 2) % 2) % 2) * 2 + (c + p % 2) % 2


def _aligned(i, n):
    return pl.multiple_of(i * n, n)


def _layer_kernel(l, groups, x_hbm, g1_ref, g2_ref, c_ref, s_ref, wk, wv, wq, wo, w1, w3, w2,
                  y_out, k_out, v_out,
                  x_ref, h_ref, u_ref, o_ref, wbuf, pbuf, qkv, obuf, acc_ref,
                  asem, wsem, psend, precv, pown, osend, orecv, oown, csem):
    me = lax.axis_index('cp')
    rows, d = x_ref.shape
    ff = u_ref.shape[1]
    seg = rows // 2
    nb = wbuf.shape[0]
    ahead = nb - 1
    wd = d // NCP
    ng = len(groups)
    nqb, bq, _ = obuf.shape
    per = bq // seg
    nseg = nqb * per
    mats = (wk, wv, wq)
    n_p = 3 * NCP
    tn = 512
    n_o, n_up, n_dn = d // tn, pl.cdiv(ff, tn // 2), d // tn
    kcs = [(k, min(d, ff - k)) for k in range(0, ff, d)]
    nk = len(kcs)


    def chunk(src, t, nrow, off, wide, part):
        slot = t % nb
        return pltpu.make_async_copy(
            src, wbuf.at[slot, pl.ds(0, nrow), pl.ds(off, wide)], wsem.at[slot, part])

    def p_chunk(gi, mat, i):
        h0, nh = groups[gi]
        p = NCP - 1 - i % NCP
        col = pl.multiple_of(_peer(p) * wd + h0 * HEAD, HEAD)
        return chunk(mat.at[l, :, pl.ds(col, nh * HEAD)], gi * n_p + i, d, 0, nh * HEAD, 0)

    def p_start(gi, i):
        for m in range(3):
            @pl.when(i // NCP == m)
            def _():
                p_chunk(gi, mats[m], i).start()

    def p_wait(gi, i):
        p_chunk(gi, mats[0], i).wait()

    t_o, t_up = ng * n_p, ng * n_p + n_o
    t_dn = t_up + n_up

    def o_chunks(j):
        return (chunk(wo.at[l, :, pl.ds(_aligned(j, tn), tn)], t_o + j, d, 0, tn, 0),)

    def up_off(j):
        return pl.multiple_of(jnp.minimum(j * (tn // 2), ff - tn // 2), HEAD)

    def up_chunks(j):
        cs = pl.ds(up_off(j), tn // 2)
        return (chunk(w1.at[l, :, cs], t_up + j, d, 0, tn // 2, 0),
                chunk(w3.at[l, :, cs], t_up + j, d, tn // 2, tn // 2, 1))

    def dn_chunks(j, kc):
        k0, kn = kcs[kc]
        return (chunk(w2.at[l, pl.ds(k0, kn), pl.ds(_aligned(j, tn), tn)],
                      t_dn + nk * j + kc, kn, 0, tn, 0),)

    def start(cs):
        for c in cs:
            c.start()

    def wait(cs):
        for c in cs:
            c.wait()

    def stream(n, begin, finish, begin_next, fn):
        def step(j, _):
            @pl.when(j + ahead < n)
            def _():
                begin(j + ahead)

            @pl.when(j + ahead >= n)
            def _():
                begin_next(j + ahead - n)
            finish(j)
            fn(j)
            return 0

        lax.fori_loop(0, n, step, 0)


    def p_pair(gi, m, p, half):
        h0, nh = groups[gi]
        dst = pl.multiple_of((me + half * (2 * NCP - 1 - 2 * me)) * seg, seg)
        return (pbuf.at[m, p, pl.ds(h0, nh), pl.ds(half * seg, seg)],
                qkv.at[m, pl.ds(h0, nh), pl.ds(dst, seg)])

    def p_remote(gi, m, p, half):
        src, dst = p_pair(gi, m, p, half)
        return pltpu.make_async_remote_copy(
            src_ref=src, dst_ref=dst, send_sem=psend.at[gi, m, p, half],
            recv_sem=precv.at[gi, m, p, half], device_id={'cp': _peer(p)}, device_id_type=MESH)

    def p_local(gi, m, half):
        src, dst = p_pair(gi, m, 0, half)
        return pltpu.make_async_copy(src, dst, pown.at[gi, m, half])

    def p_step(gi):
        h0, nh = groups[gi]

        def fn(i):
            m, p = i // NCP, NCP - 1 - i % NCP
            acc = jnp.dot(h_ref[...], wbuf[(gi * n_p + i) % nb, :, 0:nh * HEAD],
                          preferred_element_type=F32)
            for h in range(nh):
                t = acc[:, h * HEAD:(h + 1) * HEAD]
                r = t * c_ref[...] + pltpu.roll(t, HEAD // 2, 1) * s_ref[...]
                pbuf[m, p, h0 + h] = jnp.where(m == 1, t, r).astype(BF16)

            @pl.when(p > 0)
            def _():
                for half in range(2):
                    p_remote(gi, m, p, half).start()

            @pl.when(p == 0)
            def _():
                for half in range(2):
                    p_local(gi, m, half).start()

        return fn

    def p_arrive(gi):
        for m in range(3):
            for half in range(2):
                p_local(gi, m, half).wait()

        def fin(i, _):
            for half in range(2):
                p_remote(gi, i // (NCP - 1), 1 + i % (NCP - 1), half).wait_recv()
            return 0

        lax.fori_loop(0, 3 * (NCP - 1), fin, 0)

    def p_sent(gi):
        def fin(i, _):
            for half in range(2):
                p_remote(gi, i // (NCP - 1), 1 + i % (NCP - 1), half).wait_send()
            return 0

        lax.fori_loop(0, 3 * (NCP - 1), fin, 0)

    def caches(gi):
        h0, nh = groups[gi]
        hs = pl.ds(h0, nh)
        return (pltpu.make_async_copy(qkv.at[0, hs], k_out.at[hs], csem.at[gi, 0]),
                pltpu.make_async_copy(qkv.at[1, hs], v_out.at[hs], csem.at[gi, 1]))


    def half_of(sg):
        return sg // NCP

    def owner(sg):
        return sg + half_of(sg) * (2 * NCP - 1 - 2 * sg)

    def place(gi, dev, half):
        h0, nh = groups[gi]
        return o_ref.at[pl.ds(_aligned(half, seg), seg),
                        pl.ds(pl.multiple_of(dev * wd + h0 * HEAD, HEAD), nh * HEAD)]

    def o_src(gi, sg):
        h0, nh = groups[gi]
        return obuf.at[sg // per, pl.ds(_aligned(sg % per, seg), seg), pl.ds(h0 * HEAD, nh * HEAD)]

    def o_remote(gi, sg):
        return pltpu.make_async_remote_copy(
            src_ref=o_src(gi, sg), dst_ref=place(gi, me, half_of(sg)),
            send_sem=osend.at[gi, sg], recv_sem=orecv.at[gi, me, half_of(sg)],
            device_id={'cp': owner(sg)}, device_id_type=MESH)

    def o_local(gi, sg):
        return pltpu.make_async_copy(o_src(gi, sg), place(gi, me, half_of(sg)), oown.at[gi, half_of(sg)])

    def o_each(gi, lo, n, far, near):
        def one(i, _):
            sg = lo + i

            @pl.when(owner(sg) != me)
            def _():
                far(o_remote(gi, sg))

            @pl.when(owner(sg) == me)
            def _():
                near(o_local(gi, sg))
            return 0

        lax.fori_loop(0, n, one, 0)

    def o_arrive(gi):
        def fin(p, _):
            src = _peer(p)
            for half in range(2):
                pltpu.make_async_remote_copy(
                    src_ref=o_src(gi, 0), dst_ref=place(gi, src, half),
                    send_sem=osend.at[gi, 0], recv_sem=orecv.at[gi, src, half],
                    device_id={'cp': src}, device_id_type=MESH).wait_recv()
            return 0

        lax.fori_loop(1, NCP, fin, 0)


    cexp = HEAD ** -0.5 * 1.4426950408889634
    dmask = (lax.broadcasted_iota(jnp.int32, (bq, bq), 0)
             <= lax.broadcasted_iota(jnp.int32, (bq, bq), 1))

    def attention(gi):
        h0, nh = groups[gi]

        def qblock(qi, _):
            qrows = pl.ds(_aligned(qi, bq), bq)
            for i in range(nh):
                acc_ref[i] = jnp.zeros(acc_ref.shape[1:], F32)

            def block(kb, carry, diag):
                krows = pl.ds(_aligned(kb, bq), bq)
                new = []
                for i in range(nh):
                    m, den = carry[i]
                    sc = lax.dot_general(qkv[0, h0 + i, krows], qkv[2, h0 + i, qrows],
                                         (((1,), (1,)), ((), ())), preferred_element_type=F32)
                    if diag:
                        sc = jnp.where(dmask, sc, -jnp.inf)
                    mn = jnp.maximum(m, jnp.max(sc, axis=0, keepdims=True))
                    p = jnp.exp2((sc - mn) * cexp)
                    al = jnp.exp2((m - mn) * cexp)
                    den = den * al + jnp.sum(p, axis=0, keepdims=True)
                    pv = lax.dot_general(qkv[1, h0 + i, krows], p.astype(BF16),
                                         (((0,), (0,)), ((), ())), preferred_element_type=F32)
                    acc_ref[i] = acc_ref[i] * al + pv
                    new.append((mn, den))
                return tuple(new)

            init = tuple((jnp.full((1, bq), -jnp.inf, F32), jnp.zeros((1, bq), F32)) for _ in range(nh))
            carry = block(qi, init, True)
            carry = lax.fori_loop(0, qi, lambda kb, cr: block(kb, cr, False), carry)
            for i in range(nh):
                obuf[qi, :, (h0 + i) * HEAD:(h0 + i + 1) * HEAD] = (acc_ref[i] / carry[i][1]).T.astype(BF16)
            o_each(gi, qi * per, per, lambda c: c.start(), lambda c: c.start())
            return 0

        lax.fori_loop(0, nqb, qblock, 0)


    xcp = pltpu.make_async_copy(x_hbm, x_ref, asem)
    xcp.start()
    for i in range(ahead):
        p_start(0, i)
    barrier = pltpu.get_barrier_semaphore()
    for p in range(1, NCP):
        pl.semaphore_signal(barrier, inc=1, device_id={'cp': _peer(p)}, device_id_type=MESH)
    pl.semaphore_wait(barrier, NCP - 1)
    xcp.wait()
    h_ref[...] = _norm(x_ref[...], g1_ref[l:l + 1])

    for gi in range(ng):
        if gi + 1 < ng:
            begin_next = functools.partial(p_start, gi + 1)
        else:
            def begin_next(j):
                start(o_chunks(j))
        stream(n_p, functools.partial(p_start, gi), functools.partial(p_wait, gi), begin_next, p_step(gi))

    for gi in range(ng):
        p_arrive(gi)
        start(caches(gi))
        attention(gi)
    for gi in range(ng):
        o_each(gi, 0, nseg, lambda c: c.wait_send(), lambda c: c.wait())
        o_arrive(gi)

    def o_step(j):
        cs = pl.ds(_aligned(j, tn), tn)
        x_ref[:, cs] = (x_ref[:, cs].astype(F32)
                        + jnp.dot(o_ref[...], wbuf[(t_o + j) % nb, :, 0:tn],
                                  preferred_element_type=F32)).astype(BF16)

    stream(n_o, lambda j: start(o_chunks(j)), lambda j: wait(o_chunks(j)),
           lambda j: start(up_chunks(j)), o_step)
    h_ref[...] = _norm(x_ref[...], g2_ref[l:l + 1])

    def up_step(j):
        ab = jnp.dot(h_ref[...], wbuf[(t_up + j) % nb, :, 0:tn], preferred_element_type=F32)
        a, b = ab[:, :tn // 2], ab[:, tn // 2:]
        u_ref[:, pl.ds(up_off(j), tn // 2)] = (jax.nn.silu(a) * b).astype(BF16)

    def dn_next(t):
        for i in range(ahead):
            @pl.when(t == i)
            def _():
                start(dn_chunks(i // nk, i % nk))

    stream(n_up, lambda j: start(up_chunks(j)), lambda j: wait(up_chunks(j)), dn_next, up_step)

    def dn_step(j, _):
        cs = pl.ds(_aligned(j, tn), tn)
        acc = x_ref[:, cs].astype(F32)
        for kc, (k0, kn) in enumerate(kcs):
            jn, kcn = j + (kc + ahead) // nk, (kc + ahead) % nk

            @pl.when(jn < n_dn)
            def _():
                start(dn_chunks(jn, kcn))
            wait(dn_chunks(j, kc))
            acc = acc + jnp.dot(u_ref[:, k0:k0 + kn], wbuf[(t_dn + nk * j + kc) % nb, 0:kn, 0:tn],
                                preferred_element_type=F32)
        x_ref[:, cs] = acc.astype(BF16)
        return 0

    lax.fori_loop(0, n_dn, dn_step, 0)
    ycp = pltpu.make_async_copy(x_ref, y_out, asem)
    ycp.start()
    for gi in range(ng):
        p_sent(gi)
        wait(caches(gi))
    ycp.wait()


def _layer(x, g1, g2, c, s, wk, wv, wq, wo, w1, w3, w2, l):
    rows, d = x.shape
    ff = w1.shape[2]
    nh = wq.shape[2] // NCP // HEAD
    n = rows * NCP
    first = (nh + 1) // 2
    groups = ((0, first), (first, nh - first))
    ng, nb = len(groups), 3
    kv = jax.ShapeDtypeStruct((nh, n, HEAD), BF16)
    dma = pltpu.SemaphoreType.DMA
    return pl.pallas_call(
        functools.partial(_layer_kernel, l, groups),
        in_specs=[ANY] + [VM] * 4 + [ANY] * 7,
        out_specs=[ANY] * 3,
        out_shape=[jax.ShapeDtypeStruct((rows, d), BF16), kv, kv],
        scratch_shapes=[
            pltpu.VMEM((rows, d), BF16), pltpu.VMEM((rows, d), BF16), pltpu.VMEM((rows, ff), BF16),
            pltpu.VMEM((rows, d), BF16), pltpu.VMEM((nb, d, 512), BF16),
            pltpu.VMEM((3, NCP, nh, rows, HEAD), BF16), pltpu.VMEM((3, nh, n, HEAD), BF16),
            pltpu.VMEM((n // BQ, BQ, nh * HEAD), BF16), pltpu.VMEM((first, HEAD, BQ), F32),
            dma, dma((nb, 2)), dma((ng, 3, NCP, 2)), dma((ng, 3, NCP, 2)), dma((ng, 3, 2)),
            dma((ng, 2 * NCP)), dma((ng, NCP, 2)), dma((ng, 2)), dma((ng, 2)),
        ],
        compiler_params=pltpu.CompilerParams(
            vmem_limit_bytes=VLIM, collective_id=l, has_side_effects=True),
        name=f'layer{l}',
    )(x, g1, g2, c, s, wk, wv, wq, wo, w1, w3, w2)


def solution(mesh):
    act = P(('req', 'cp'), None)
    cache = P(None, 'req', 'cp', None)

    def body(x, pos, g1, g2, wq, wk, wv, wo, w1, w3, w2):
        c, s = _tables(pos)
        ks, vs = [], []
        for l in range(wq.shape[0]):
            x, k, v = _layer(x, g1, g2, c, s, wk, wv, wq, wo, w1, w3, w2, l)
            ks.append(k)
            vs.append(v)
        return x, jnp.stack(ks).transpose(0, 2, 1, 3), jnp.stack(vs).transpose(0, 2, 1, 3)

    return jax.shard_map(body, mesh=mesh, in_specs=(act, P(('req', 'cp'))) + (P(),) * 9,
                         out_specs=(act, cache, cache), check_vma=False)
```

time: 1760 us -> 553 us (0.31); the launches traced: 1740 us -> 553 us
  matrix products: 773 us -> 0 us
  Pallas kernels: 0 us -> 540 us
  local copies, waits for them, and re-layouts: 508 us -> 1.5 us
  waiting for transfers between devices: 359 us -> 0 us
  other arithmetic: 61.5 us -> 10.4 us
    dot_general x174 -> x0, matrix products: 773 us -> none  [the longest x80 132 us: one(): jnp.einsum('qd,kd->qk', qh, kh, preferred_element_type=F32) * HEAD ** (-0.5)]
    pallas_call x0 -> x2, Pallas kernels: none -> 540 us  [_layer(): pl.pallas_call(functools.partial(_layer_kernel, l, groups), in_specs=[ANY...]
    dot_general x6 -> x0, local copies, waits for them, and re-layouts: 402 us -> none  [the longest x3 203 us: body(): jnp.dot(h, wq[l], preferred_element_type=F32).reshape(s_dev, nh, HEAD)]
    all_to_all x2 -> x0, waiting for transfers between devices: 180 us -> none  [the longest x1 100 us: body(): kc = _natural(lax.all_to_all(jnp.stack(kl), 'cp', 2, 1, tiled=True), ncp)]
    all_gather x4 -> x0, waiting for transfers between devices: 178 us -> none  [the longest x2 106 us: body(): vg = lax.all_gather(v, 'cp', tiled=True)]
    reduce_sum x81 -> x0, other arithmetic: 37.2 us -> none  [the longest x80 34.9 us: one(): p = jax.nn.softmax(jnp.where(mask, sc, -jnp.inf), axis=-1).astype(BF16)]
    dynamic_update_slice x160 -> x0, local copies, waits for them, and re-layouts: 34.6 us -> none  [_attention(): lax.map(one, (q.transpose(1, 0, 2), kg.transpose(1, 0, 2), vg.transpose(1...]
    unnamed x66 -> x7, local copies, waits for them, and re-layouts: 28.4 us -> 1.5 us
  transfers between devices with their start and end apart: 6 -> 0, of which waited for: 4 -> 0; matrix products, arithmetic and copies ran while one was open for 16% -> 0% of each run, Pallas kernels for 0% -> 0%
where the time goes in v2:
time: 553 us
  Pallas kernels  540 us (98%)
  other arithmetic  10.4 us (2%)
    pallas_call x2, Pallas kernels, _layer(): pl.pallas_call(functools.partial(_layer_kernel, l, groups), in_specs=[ANY...  540 us

profile of v2, /device:TPU:0, one launch (start us, length us, event | category | flops | bytes accessed | tf_op | source)
XLA Modules:
  0.0 552.8 jit_solution(11992887061130962925)
XLA Ops:
  0.6 0.7 convert_element_type.3
  1.3 0.5 fusion
  1.9 0.8 pad_maximum_fusion
  2.7 272.7 %layer0.1 = (bf16[256,5120]{1,0:T(8,128)(2,1)}, bf16[5,2048,128]{2,1,0:T(8,128)(2,1)}, bf16[5,2048,128]{2,1,0:T(8,128)(2,1)}) custom-call(bf16[256,5120]{1,0:T(8,128)(2,1)} %x_hbm.1, bf16[2,5120]{1,0:T(2,128)(2,1)} %g1_ref.3, bf16[2,5120]{1,0:T(2,128)(2,1)} %g2_ref.3, f32[256,128]{1,0:T(8,128)} %get-tuple-element.18.c_ref, ...), custom_call_target="tpu_custom_call" | custom-call | tf_op jit(solution)/shard_map/layer0/pallas_call | solution.py:376
  275.4 267.5 %layer1.1 = (bf16[256,5120]{1,0:T(8,128)(2,1)}, bf16[5,2048,128]{2,1,0:T(8,128)(2,1)}, bf16[5,2048,128]{2,1,0:T(8,128)(2,1)}) custom-call(bf16[256,5120]{1,0:T(8,128)(2,1)} %get-tuple-element.9.x_hbm, bf16[2,5120]{1,0:T(2,128)(2,1)} %g1_ref.3, bf16[2,5120]{1,0:T(2,128)(2,1)} %g2_ref.3, f32[256,128]{1,0:T(8,128)} %get-tuple-element.18.c_ref, ...), custom_call_target="tpu_custom_call" | custom-call | tf_op jit(solution)/shard_map/layer1/pallas_call | solution.py:376
  543.0 0.0 copy-start
  543.0 0.0 copy-start.1
  543.0 5.5 maximum_bitcast_fusion
  548.5 0.0 copy-done
  548.5 0.0 copy-done.1
  548.5 0.0 copy-start.2
  548.5 2.8 maximum_bitcast_fusion.1
  551.3 0.0 copy-done.2
  551.3 1.5 copy.15
  (1 shorter events, 0.0 us)
Async XLA Ops:
  543.0 5.5 %copy-start = (bf16[5,2048,128]{2,1,0:T(8,128)(2,1)S(1)}, bf16[5,2048,128]{2,1,0:T(8,128)(2,1)}, u32[]{:S(2)}) copy-start(bf16[5,2048,128]{2,1,0:T(8,128)(2,1)} %get-tuple-element.13) | copy-start | bytes 7864324
  543.0 5.5 %copy-start.1 = (bf16[5,2048,128]{2,1,0:T(8,128)(2,1)S(1)}, bf16[5,2048,128]{2,1,0:T(8,128)(2,1)}, u32[]{:S(2)}) copy-start(bf16[5,2048,128]{2,1,0:T(8,128)(2,1)} %get-tuple-element.14) | copy-start | bytes 7864324
  548.5 2.8 copy-start.2

commit v3 on v2

--- a/solution.py
+++ b/solution.py
@@ -42,10 +42,10 @@
     return pl.multiple_of(i * n, n)
 
 
-def _layer_kernel(l, groups, x_hbm, g1_ref, g2_ref, c_ref, s_ref, wk, wv, wq, wo, w1, w3, w2,
+def _layers_kernel(nl, groups, x_hbm, g1_ref, g2_ref, c_ref, s_ref, wk, wv, wq, wo, w1, w3, w2,
                   y_out, k_out, v_out,
                   x_ref, h_ref, u_ref, o_ref, wbuf, pbuf, qkv, obuf, acc_ref,
-                  asem, wsem, psend, precv, pown, osend, orecv, oown, csem):
+                  asem, wsem, psend, precv, pown, osend, orecv, oown, csem, free):
     me = lax.axis_index('cp')
     rows, d = x_ref.shape
     ff = u_ref.shape[1]
@@ -70,39 +70,22 @@
         return pltpu.make_async_copy(
             src, wbuf.at[slot, pl.ds(0, nrow), pl.ds(off, wide)], wsem.at[slot, part])
 
-    def p_chunk(gi, mat, i):
+    t_layer = ng * n_p + n_o + n_up + n_dn * nk
+
+    def p_chunk(l, gi, mat, i):
         h0, nh = groups[gi]
         p = NCP - 1 - i % NCP
         col = pl.multiple_of(_peer(p) * wd + h0 * HEAD, HEAD)
-        return chunk(mat.at[l, :, pl.ds(col, nh * HEAD)], gi * n_p + i, d, 0, nh * HEAD, 0)
-
-    def p_start(gi, i):
+        return chunk(mat.at[l, :, pl.ds(col, nh * HEAD)], l * t_layer + gi * n_p + i, d, 0, nh * HEAD, 0)
+
+    def p_start(l, gi, i):
         for m in range(3):
             @pl.when(i // NCP == m)
             def _():
-                p_chunk(gi, mats[m], i).start()
-
-    def p_wait(gi, i):
-        p_chunk(gi, mats[0], i).wait()
-
-    t_o, t_up = ng * n_p, ng * n_p + n_o
-    t_dn = t_up + n_up
-
-    def o_chunks(j):
-        return (chunk(wo.at[l, :, pl.ds(_aligned(j, tn), tn)], t_o + j, d, 0, tn, 0),)
-
-    def up_off(j):
-        return pl.multiple_of(jnp.minimum(j * (tn // 2), ff - tn // 2), HEAD)
-
-    def up_chunks(j):
-        cs = pl.ds(up_off(j), tn // 2)
-        return (chunk(w1.at[l, :, cs], t_up + j, d, 0, tn // 2, 0),
-                chunk(w3.at[l, :, cs], t_up + j, d, tn // 2, tn // 2, 1))
-
-    def dn_chunks(j, kc):
-        k0, kn = kcs[kc]
-        return (chunk(w2.at[l, pl.ds(k0, kn), pl.ds(_aligned(j, tn), tn)],
-                      t_dn + nk * j + kc, kn, 0, tn, 0),)
+                p_chunk(l, gi, mats[m], i).start()
+
+    def p_wait(l, gi, i):
+        p_chunk(l, gi, mats[0], i).wait()
 
     def start(cs):
         for c in cs:
@@ -144,30 +127,6 @@
         src, dst = p_pair(gi, m, 0, half)
         return pltpu.make_async_copy(src, dst, pown.at[gi, m, half])
 
-    def p_step(gi):
-        h0, nh = groups[gi]
-
-        def fn(i):
-            m, p = i // NCP, NCP - 1 - i % NCP
-            acc = jnp.dot(h_ref[...], wbuf[(gi * n_p + i) % nb, :, 0:nh * HEAD],
-                          preferred_element_type=F32)
-            for h in range(nh):
-                t = acc[:, h * HEAD:(h + 1) * HEAD]
-                r = t * c_ref[...] + pltpu.roll(t, HEAD // 2, 1) * s_ref[...]
-                pbuf[m, p, h0 + h] = jnp.where(m == 1, t, r).astype(BF16)
-
-            @pl.when(p > 0)
-            def _():
-                for half in range(2):
-                    p_remote(gi, m, p, half).start()
-
-            @pl.when(p == 0)
-            def _():
-                for half in range(2):
-                    p_local(gi, m, half).start()
-
-        return fn
-
     def p_arrive(gi):
         for m in range(3):
             for half in range(2):
@@ -187,12 +146,6 @@
             return 0
 
         lax.fori_loop(0, 3 * (NCP - 1), fin, 0)
-
-    def caches(gi):
-        h0, nh = groups[gi]
-        hs = pl.ds(h0, nh)
-        return (pltpu.make_async_copy(qkv.at[0, hs], k_out.at[hs], csem.at[gi, 0]),
-                pltpu.make_async_copy(qkv.at[1, hs], v_out.at[hs], csem.at[gi, 1]))
 
 
     def half_of(sg):
@@ -292,89 +245,157 @@
     xcp = pltpu.make_async_copy(x_hbm, x_ref, asem)
     xcp.start()
     for i in range(ahead):
-        p_start(0, i)
+        p_start(0, 0, i)
     barrier = pltpu.get_barrier_semaphore()
     for p in range(1, NCP):
         pl.semaphore_signal(barrier, inc=1, device_id={'cp': _peer(p)}, device_id_type=MESH)
     pl.semaphore_wait(barrier, NCP - 1)
     xcp.wait()
-    h_ref[...] = _norm(x_ref[...], g1_ref[l:l + 1])
-
-    for gi in range(ng):
-        if gi + 1 < ng:
-            begin_next = functools.partial(p_start, gi + 1)
-        else:
-            def begin_next(j):
-                start(o_chunks(j))
-        stream(n_p, functools.partial(p_start, gi), functools.partial(p_wait, gi), begin_next, p_step(gi))
-
-    for gi in range(ng):
-        p_arrive(gi)
-        start(caches(gi))
-        attention(gi)
-    for gi in range(ng):
-        o_each(gi, 0, nseg, lambda c: c.wait_send(), lambda c: c.wait())
-        o_arrive(gi)
-
-    def o_step(j):
-        cs = pl.ds(_aligned(j, tn), tn)
-        x_ref[:, cs] = (x_ref[:, cs].astype(F32)
-                        + jnp.dot(o_ref[...], wbuf[(t_o + j) % nb, :, 0:tn],
-                                  preferred_element_type=F32)).astype(BF16)
-
-    stream(n_o, lambda j: start(o_chunks(j)), lambda j: wait(o_chunks(j)),
-           lambda j: start(up_chunks(j)), o_step)
-    h_ref[...] = _norm(x_ref[...], g2_ref[l:l + 1])
-
-    def up_step(j):
-        ab = jnp.dot(h_ref[...], wbuf[(t_up + j) % nb, :, 0:tn], preferred_element_type=F32)
-        a, b = ab[:, :tn // 2], ab[:, tn // 2:]
-        u_ref[:, pl.ds(up_off(j), tn // 2)] = (jax.nn.silu(a) * b).astype(BF16)
-
-    def dn_next(t):
-        for i in range(ahead):
-            @pl.when(t == i)
-            def _():
-                start(dn_chunks(i // nk, i % nk))
-
-    stream(n_up, lambda j: start(up_chunks(j)), lambda j: wait(up_chunks(j)), dn_next, up_step)
-
-    def dn_step(j, _):
-        cs = pl.ds(_aligned(j, tn), tn)
-        acc = x_ref[:, cs].astype(F32)
-        for kc, (k0, kn) in enumerate(kcs):
-            jn, kcn = j + (kc + ahead) // nk, (kc + ahead) % nk
-
-            @pl.when(jn < n_dn)
-            def _():
-                start(dn_chunks(jn, kcn))
-            wait(dn_chunks(j, kc))
-            acc = acc + jnp.dot(u_ref[:, k0:k0 + kn], wbuf[(t_dn + nk * j + kc) % nb, 0:kn, 0:tn],
-                                preferred_element_type=F32)
-        x_ref[:, cs] = acc.astype(BF16)
-        return 0
-
-    lax.fori_loop(0, n_dn, dn_step, 0)
+
+    def layer(l):
+        base = l * t_layer
+        t_o = base + ng * n_p
+        t_up = t_o + n_o
+        t_dn = t_up + n_up
+
+        def o_chunks(j):
+            return (chunk(wo.at[l, :, pl.ds(_aligned(j, tn), tn)], t_o + j, d, 0, tn, 0),)
+
+        def up_off(j):
+            return pl.multiple_of(jnp.minimum(j * (tn // 2), ff - tn // 2), HEAD)
+
+        def up_chunks(j):
+            cs = pl.ds(up_off(j), tn // 2)
+            return (chunk(w1.at[l, :, cs], t_up + j, d, 0, tn // 2, 0),
+                    chunk(w3.at[l, :, cs], t_up + j, d, tn // 2, tn // 2, 1))
+
+        def dn_chunks(j, kc):
+            k0, kn = kcs[kc]
+            return (chunk(w2.at[l, pl.ds(k0, kn), pl.ds(_aligned(j, tn), tn)],
+                          t_dn + nk * j + kc, kn, 0, tn, 0),)
+
+        def p_step(gi):
+            h0, nh = groups[gi]
+
+            def fn(i):
+                m, p = i // NCP, NCP - 1 - i % NCP
+                acc = jnp.dot(h_ref[...], wbuf[(base + gi * n_p + i) % nb, :, 0:nh * HEAD],
+                              preferred_element_type=F32)
+                for h in range(nh):
+                    t = acc[:, h * HEAD:(h + 1) * HEAD]
+                    r = t * c_ref[...] + pltpu.roll(t, HEAD // 2, 1) * s_ref[...]
+                    pbuf[m, p, h0 + h] = jnp.where(m == 1, t, r).astype(BF16)
+
+                @pl.when(p > 0)
+                def _():
+                    for half in range(2):
+                        p_remote(gi, m, p, half).start()
+
+                @pl.when(p == 0)
+                def _():
+                    for half in range(2):
+                        p_local(gi, m, half).start()
+
+            return fn
+
+        def caches(gi):
+            h0, nh = groups[gi]
+            hs = pl.ds(h0, nh)
+            return (pltpu.make_async_copy(qkv.at[0, hs], k_out.at[l, hs], csem.at[gi, 0]),
+                    pltpu.make_async_copy(qkv.at[1, hs], v_out.at[l, hs], csem.at[gi, 1]))
+
+        h_ref[...] = _norm(x_ref[...], g1_ref[l:l + 1])
+        if l > 0:
+            pl.semaphore_wait(free, NCP - 1)
+
+        for gi in range(ng):
+            if gi + 1 < ng:
+                begin_next = functools.partial(p_start, l, gi + 1)
+            else:
+                def begin_next(j):
+                    start(o_chunks(j))
+            stream(n_p, functools.partial(p_start, l, gi), functools.partial(p_wait, l, gi), begin_next, p_step(gi))
+
+        for gi in range(ng):
+            p_arrive(gi)
+            start(caches(gi))
+            if gi + 1 == ng:
+                for gj in range(ng):
+                    wait(caches(gj))
+            attention(gi)
+        if l + 1 < nl:
+            for p in range(1, NCP):
+                pl.semaphore_signal(free, inc=1, device_id={'cp': _peer(p)}, device_id_type=MESH)
+        for gi in range(ng):
+            o_each(gi, 0, nseg, lambda c: c.wait_send(), lambda c: c.wait())
+            o_arrive(gi)
+
+        def o_step(j):
+            cs = pl.ds(_aligned(j, tn), tn)
+            x_ref[:, cs] = (x_ref[:, cs].astype(F32)
+                            + jnp.dot(o_ref[...], wbuf[(t_o + j) % nb, :, 0:tn],
+                                      preferred_element_type=F32)).astype(BF16)
+
+        stream(n_o, lambda j: start(o_chunks(j)), lambda j: wait(o_chunks(j)),
+               lambda j: start(up_chunks(j)), o_step)
+        h_ref[...] = _norm(x_ref[...], g2_ref[l:l + 1])
+
+        def up_step(j):
+            ab = jnp.dot(h_ref[...], wbuf[(t_up + j) % nb, :, 0:tn], preferred_element_type=F32)
+            a, b = ab[:, :tn // 2], ab[:, tn // 2:]
+            u_ref[:, pl.ds(up_off(j), tn // 2)] = (jax.nn.silu(a) * b).astype(BF16)
+
+        def dn_next(t):
+            for i in range(ahead):
+                @pl.when(t == i)
+                def _():
+                    start(dn_chunks(i // nk, i % nk))
+
+        stream(n_up, lambda j: start(up_chunks(j)), lambda j: wait(up_chunks(j)), dn_next, up_step)
+
+        def dn_step(j, _):
+            cs = pl.ds(_aligned(j, tn), tn)
+            acc = x_ref[:, cs].astype(F32)
+            for kc, (k0, kn) in enumerate(kcs):
+                jn, kcn = j + (kc + ahead) // nk, (kc + ahead) % nk
+
+                @pl.when(jn < n_dn)
+                def _():
+                    start(dn_chunks(jn, kcn))
+                if l + 1 < nl:
+                    @pl.when(jn >= n_dn)
+                    def _():
+                        p_start(l + 1, 0, nk * (jn - n_dn) + kcn)
+                wait(dn_chunks(j, kc))
+                acc = acc + jnp.dot(u_ref[:, k0:k0 + kn], wbuf[(t_dn + nk * j + kc) % nb, 0:kn, 0:tn],
+                                    preferred_element_type=F32)
+            x_ref[:, cs] = acc.astype(BF16)
+            return 0
+
+        lax.fori_loop(0, n_dn, dn_step, 0)
+        for gi in range(ng):
+            p_sent(gi)
+
+    for l in range(nl):
+        layer(l)
     ycp = pltpu.make_async_copy(x_ref, y_out, asem)
     ycp.start()
-    for gi in range(ng):
-        p_sent(gi)
-        wait(caches(gi))
     ycp.wait()
 
 
-def _layer(x, g1, g2, c, s, wk, wv, wq, wo, w1, w3, w2, l):
+def _layers(x, g1, g2, c, s, wk, wv, wq, wo, w1, w3, w2):
     rows, d = x.shape
+    nl = wq.shape[0]
     ff = w1.shape[2]
     nh = wq.shape[2] // NCP // HEAD
     n = rows * NCP
     first = (nh + 1) // 2
     groups = ((0, first), (first, nh - first))
-    ng, nb = len(groups), 3
-    kv = jax.ShapeDtypeStruct((nh, n, HEAD), BF16)
+    ng, nb = len(groups), 4
+    kv = jax.ShapeDtypeStruct((nl, nh, n, HEAD), BF16)
     dma = pltpu.SemaphoreType.DMA
     return pl.pallas_call(
-        functools.partial(_layer_kernel, l, groups),
+        functools.partial(_layers_kernel, nl, groups),
         in_specs=[ANY] + [VM] * 4 + [ANY] * 7,
         out_specs=[ANY] * 3,
         out_shape=[jax.ShapeDtypeStruct((rows, d), BF16), kv, kv],
@@ -384,11 +405,11 @@
             pltpu.VMEM((3, NCP, nh, rows, HEAD), BF16), pltpu.VMEM((3, nh, n, HEAD), BF16),
             pltpu.VMEM((n // BQ, BQ, nh * HEAD), BF16), pltpu.VMEM((first, HEAD, BQ), F32),
             dma, dma((nb, 2)), dma((ng, 3, NCP, 2)), dma((ng, 3, NCP, 2)), dma((ng, 3, 2)),
-            dma((ng, 2 * NCP)), dma((ng, NCP, 2)), dma((ng, 2)), dma((ng, 2)),
+            dma((ng, 2 * NCP)), dma((ng, NCP, 2)), dma((ng, 2)), dma((ng, 2)), pltpu.SemaphoreType.REGULAR,
         ],
         compiler_params=pltpu.CompilerParams(
-            vmem_limit_bytes=VLIM, collective_id=l, has_side_effects=True),
-        name=f'layer{l}',
+            vmem_limit_bytes=VLIM, collective_id=0, has_side_effects=True),
+        name='layers',
     )(x, g1, g2, c, s, wk, wv, wq, wo, w1, w3, w2)
 
 
@@ -398,12 +419,8 @@
 
     def body(x, pos, g1, g2, wq, wk, wv, wo, w1, w3, w2):
         c, s = _tables(pos)
-        ks, vs = [], []
-        for l in range(wq.shape[0]):
-            x, k, v = _layer(x, g1, g2, c, s, wk, wv, wq, wo, w1, w3, w2, l)
-            ks.append(k)
-            vs.append(v)
-        return x, jnp.stack(ks).transpose(0, 2, 1, 3), jnp.stack(vs).transpose(0, 2, 1, 3)
+        x, k, v = _layers(x, g1, g2, c, s, wk, wv, wq, wo, w1, w3, w2)
+        return x, k.transpose(0, 2, 1, 3), v.transpose(0, 2, 1, 3)
 
     return jax.shard_map(body, mesh=mesh, in_specs=(act, P(('req', 'cp'))) + (P(),) * 9,
                          out_specs=(act, cache, cache), check_vma=False)

time: 553 us -> 545 us (0.986)
  local copies, waits for them, and re-layouts: 1.5 us -> 13.9 us
  Pallas kernels: 540 us -> 528 us
  other arithmetic: 10.4 us -> 2.07 us
    pallas_call x2 -> x1, Pallas kernels: 540 us -> 528 us  [_layers(): pl.pallas_call(functools.partial(_layers_kernel, nl, groups), in_specs=[A...]
    unnamed x7 -> x3, local copies, waits for them, and re-layouts: 1.5 us -> 13.9 us
    transpose x2 -> x0, other arithmetic: 8.33 us -> none  [the longest x1 5.52 us: body(): jnp.stack(ks).transpose(0, 2, 1, 3)]
where the time goes in v3:
time: 545 us; the launch traced here: 544 us
  Pallas kernels  528 us (97%)
  local copies, waits for them, and re-layouts  13.9 us (3%)
    pallas_call x1, Pallas kernels, _layers(): pl.pallas_call(functools.partial(_layers_kernel, nl, groups), in_specs=[A...  528 us
    unnamed x3, local copies, waits for them, and re-layouts  13.9 us

profile of v3, /device:TPU:0, one launch (start us, length us, event | category | flops | bytes accessed | tf_op | source)
XLA Modules:
  0.0 544.4 jit_solution(13415507800791151617)
XLA Ops:
  0.6 0.7 convert_element_type.3
  1.3 0.5 fusion
  1.9 0.8 pad_maximum_fusion
  2.7 527.8 %layers.1 = (bf16[256,5120]{1,0:T(8,128)(2,1)}, bf16[2,5,2048,128]{3,2,1,0:T(8,128)(2,1)}, bf16[2,5,2048,128]{3,2,1,0:T(8,128)(2,1)}) custom-call(bf16[256,5120]{1,0:T(8,128)(2,1)} %x_hbm.1, bf16[2,5120]{1,0:T(2,128)(2,1)} %g1_ref.1, bf16[2,5120]{1,0:T(2,128)(2,1)} %g2_ref.1, f32[256,128]{1,0:T(8,128)} %get-tuple-element.12.c_ref, ...), custom_call_target="tpu_custom_call" | custom-call | tf_op jit(solution)/shard_map/layers/pallas_call | solution.py:397
  530.5 3.4 copy.17
  533.9 5.2 copy.18
  539.2 5.2 copy.19
  (1 shorter events, 0.0 us)
